TPU v7x, 8 devices: a whole 2x2x1 slice. The times are simulated.
8 devices in a mesh: dp: 2 (over y, z), tp: 4 (over x, core).
Axes of the slice: x: 2, y: 2, z: 1, core: 2. Of those that a mesh axis runs over, the one named last changes fastest.
Arguments:
- x: bfloat16 [4096, 2048], P('dp'), parts along dimension 0
- dy: bfloat16 [4096, 2048], P('dp'), parts along dimension 0
- gate: bfloat16 [4096, 8192], P('dp', 'tp'), parts along dimension 0
- up: bfloat16 [4096, 8192], P('dp', 'tp'), parts along dimension 0
- w_gate: bfloat16 [2048, 8192], P(None, 'tp')
- w_up: bfloat16 [2048, 8192], P(None, 'tp')
- w_down: bfloat16 [8192, 2048], P('tp')
Outputs:
- output 1: bfloat16 [4096, 2048], P('dp'), parts along dimension 0
- output 2: bfloat16 [4096, 8192], P('dp', 'tp'), parts along dimension 0
- output 3: bfloat16 [4096, 8192], P('dp', 'tp'), parts along dimension 0
- output 4: bfloat16 [16384, 2048], P(('dp', 'tp')), parts along dimension 0
There are 2 independent parts. A program takes and returns all parts, laid end to end along the dimension named above; an argument that names none is the same for every part.
All inputs are finite; a program needn't handle non-finite values.
Results may differ from a plain program's by a relative error of at most 0.012.
Values are sent between devices in bfloat16 or wider.
A program may use at most 2 GiB of HBM per device.

v0:
```python
import jax
import jax.numpy as jnp
from jax import lax
from jax.sharding import PartitionSpec as P


def act(gate, up):
    return jax.nn.silu(gate) * up


def solution(mesh):
    def step(x, dy, gate, up, w_gate, w_up, w_down):
        hidden, back = jax.vjp(act, gate.astype(jnp.float32), up.astype(jnp.float32))
        d_hidden = jnp.dot(dy, w_down.T, preferred_element_type=jnp.float32)
        d_gate, d_up = (g.astype(jnp.bfloat16) for g in back(d_hidden))
        term = jnp.dot(d_gate, w_gate.T, preferred_element_type=jnp.float32) + jnp.dot(d_up, w_up.T, preferred_element_type=jnp.float32)
        dx = lax.psum(term.astype(jnp.bfloat16), "tp")
        dw_gate = jnp.dot(x.T, d_gate, preferred_element_type=jnp.float32)
        dw_up = jnp.dot(x.T, d_up, preferred_element_type=jnp.float32)
        dw_down = jnp.dot(hidden.astype(jnp.bfloat16).T, dy, preferred_element_type=jnp.float32)
        return dx, *(g.astype(jnp.bfloat16) for g in (dw_gate, dw_up, dw_down))

    tokens, columns, rows = P("dp", None), P(None, "tp"), P("tp", None)
    return jax.shard_map(
        step,
        mesh=mesh,
        in_specs=(tokens, tokens, P("dp", "tp"), P("dp", "tp"), columns, columns, rows),
        out_specs=(tokens, P("dp", "tp"), P("dp", "tp"), P(("dp", "tp"), None)),
        check_vma=False,
    )
```

profile of v0, /device:TPU:0, one launch (start us, length us, event | category | flops | bytes accessed | tf_op | source)
XLA Modules:
  0.0 254.9 jit_solution(1779376151076729711)
XLA Ops:
  7.2 0.0 all-reduce.2.cloned.1.call-start
  7.2 32.5 %multiply_convert_fusion = (bf16[2048,2048]{1,0:T(8,128)(2,1)}, bf16[2048,2048]{1,0:T(8,128)(2,1)}) fusion(bf16[2048,2048]{1,0:T(8,128)(2,1)} %param.9, bf16[2048,2048]{1,0:T(8,128)(2,1)} %param.10, bf16[2048,2048]{1,0:T(8,128)(2,1)} %param.8, bf16[2048,2048]{1,0:T(8,128)(2,1)} %param.13), kind=kOutput, calls=%fused_computation.14 | convolution fusion | flops 17246978048 | bytes 50331648 | tf_op jit(solution)/shard_map/dot_general | solution.py:14
  39.7 24.4 %fusion.13 = f32[2048,2048]{1,0:T(8,128)} fusion(bf16[2048,2048]{1,0:T(8,128)(2,1)} %get-tuple-element.9, bf16[2048,2048]{1,0:T(8,128)(2,1)} %param.11), kind=kOutput, calls=%fused_computation.20 | convolution fusion | flops 17179869184 | bytes 33554432 | tf_op jit(solution)/shard_map/dot_general | solution.py:16
  64.0 25.5 %add_convert_fusion = bf16[2048,2048]{1,0:T(8,128)(2,1)} fusion(f32[2048,2048]{1,0:T(8,128)} %fusion.13, bf16[2048,2048]{1,0:T(8,128)(2,1)} %get-tuple-element.8, bf16[2048,2048]{1,0:T(8,128)(2,1)} %param.12), kind=kOutput, calls=%fused_computation.13 | convolution fusion | flops 17188257792 | bytes 41943040 | tf_op jit(solution)/shard_map/dot_general | solution.py:16
  89.5 0.0 all-reduce.2.cloned.1.call-update
  89.5 23.8 %convert_bitcast_fusion.1 = bf16[2048,2048]{0,1:T(8,128)(2,1)} fusion(bf16[2048,2048]{1,0:T(8,128)(2,1)} %get-tuple-element.9, bf16[2048,2048]{1,0:T(8,128)(2,1)} %param.7), kind=kOutput, calls=%fused_computation.17 | convolution fusion | flops 17184063488 | bytes 25165824 | tf_op jit(solution)/shard_map/dot_general | solution.py:18
  113.3 23.7 %convert_bitcast_fusion = bf16[2048,2048]{0,1:T(8,128)(2,1)} fusion(bf16[2048,2048]{1,0:T(8,128)(2,1)} %get-tuple-element.8, bf16[2048,2048]{1,0:T(8,128)(2,1)} %param.7), kind=kOutput, calls=%fused_computation.16 | convolution fusion | flops 17184063488 | bytes 25165824 | tf_op jit(solution)/shard_map/dot_general | solution.py:19
  137.0 12.2 %copy.11 = bf16[2048,2048]{1,0:T(8,128)(2,1)} copy(bf16[2048,2048]{0,1:T(8,128)(2,1)} %convert_bitcast_fusion.1) | data formatting | bytes 16777216
  149.3 12.2 %copy.12 = bf16[2048,2048]{1,0:T(8,128)(2,1)} copy(bf16[2048,2048]{0,1:T(8,128)(2,1)} %convert_bitcast_fusion) | data formatting | bytes 16777216
  161.5 26.5 %fusion.9 = bf16[2048,2048]{1,0:T(8,128)(2,1)} fusion(bf16[2048,2048]{1,0:T(8,128)(2,1)} %param.8, bf16[2048,2048]{1,0:T(8,128)(2,1)} %param.10, bf16[2048,2048]{1,0:T(8,128)(2,1)} %param.9), kind=kOutput, calls=%fused_computation.18 | convolution fusion | flops 17217617920 | bytes 33554432 | tf_op jit(solution)/shard_map/dot_general | solution.py:20
  188.0 51.6 %all-reduce.2.cloned.1.call-done = bf16[2048,2048]{1,0:T(8,128)(2,1)} async-done(((bf16[2048,2048]{1,0:T(8,128)(2,1)}), bf16[2048,2048]{1,0:T(8,128)(2,1)}) %all-reduce.2.cloned.1.call-update) | async-done | bytes 8388624 | tf_op jit(solution)/shard_map/psum | solution.py:17
  239.6 8.4 %copy.14 = bf16[2048,2048]{1,0:T(8,128)(2,1)} copy(bf16[2048,2048]{1,0:T(8,128)(2,1)} %all-reduce.2.cloned.1.call-done) | data formatting | bytes 16777216
Async XLA Ops:
  7.2 232.5 %all-reduce.2.cloned.1.call-start = ((), (), s32[]{:S(2)}) async-start(), calls=%async_computation | async-start | bytes 16777216 | tf_op jit(solution)/shard_map/psum | solution.py:17
Sparse Core Ops, SparseCore 0:
  89.6 149.9 all-reduce.1
where the time goes:
time: 256 us; the launch traced here: 255 us
  matrix products  156 us (61%)
  waiting for transfers between devices  51.6 us (20%)
  local copies, waits for them, and re-layouts  32.9 us (13%)
  between operations  14 us (5%)
    psum x1, waiting for transfers between devices, step(): dx = lax.psum(term.astype(jnp.bfloat16), 'tp')  51.6 us
    unnamed x3, local copies, waits for them, and re-layouts  32.9 us
    dot_general x1, matrix products, step(): d_hidden = jnp.dot(dy, w_down.T, preferred_element_type=jnp.float32)  32.5 us
    dot_general x1, matrix products, step(): jnp.dot(hidden.astype(jnp.bfloat16).T, dy, preferred_element_type=jnp.flo...  26.5 us
    dot_general x1, matrix products, step(): jnp.dot(d_up, w_up.T, preferred_element_type=jnp.float32)  25.5 us
    dot_general x1, matrix products, step(): jnp.dot(d_gate, w_gate.T, preferred_element_type=jnp.float32)  24.4 us
    dot_general x1, matrix products, step(): dw_gate = jnp.dot(x.T, d_gate, preferred_element_type=jnp.float32)  23.8 us
    dot_general x1, matrix products, step(): dw_up = jnp.dot(x.T, d_up, preferred_element_type=jnp.float32)  23.7 us
  transfers between devices with their start and end apart: 1, of which 1 were waited for; matrix products, arithmetic and copies ran while one was open for 39% of the time, Pallas kernels for 0%

commit v1 on v0

v1 whole, which is shorter than its diff:
```python
import jax
import jax.numpy as jnp
from jax import lax
from jax.experimental import pallas as pl
from jax.experimental.pallas import tpu as pltpu
from jax.sharding import PartitionSpec as P

ROWS = 2048
D = 2048
F = 2048
R = 256
C = ROWS // R
H = D // 2
NX = 3
LATE = ROWS - NX * R
DONE_AT = {3: 0, 4: 1}
MESH = pl.DeviceIdType.MESH
NT = (((1,), (1,)), ((), ()))
TN = (((0,), (0,)), ((), ()))
BF = jnp.bfloat16


def dot(a, b, dims):
    return lax.dot_general(a, b, dims, preferred_element_type=jnp.float32)


def back_kernel(
    dy, gate, up, wd, wg, wu,
    dg_o, du_o, hid_o, dx_o, late_o,
    wd_v, wgu_v, dy_v, g_v, u_v, acc, dgu_v, hid_v, term_v, got_v, sum_v, cross_v,
    wd_s, wgu_s, in_s, out_s, p1s, p1r, xs, xr, p3s, p3r, f_s, late_s,
):
    me = lax.axis_index("tp")
    core = lax.rem(me, 2)
    partner = me + 1 - 2 * core
    across = lax.rem(me + 2, 4)

    def load(r, slot):
        rows = pl.ds(pl.multiple_of(r * R, R), R)
        return [
            pltpu.make_async_copy(src.at[rows, :], dst.at[slot], in_s.at[slot, k])
            for k, (src, dst) in enumerate(((dy, dy_v), (gate, g_v), (up, u_v)))
        ]

    def store(r, slot):
        rows = pl.ds(pl.multiple_of(r * R, R), R)
        return [
            pltpu.make_async_copy(dgu_v.at[slot, :, pl.ds(0, F)], dg_o.at[rows, :], out_s.at[slot, 0]),
            pltpu.make_async_copy(dgu_v.at[slot, :, pl.ds(F, F)], du_o.at[rows, :], out_s.at[slot, 1]),
            pltpu.make_async_copy(hid_v.at[slot], hid_o.at[rows, :], out_s.at[slot, 2]),
        ]

    def wd_load(n):
        rows = pl.ds(n * (F // 4), F // 4)
        return pltpu.make_async_copy(wd.at[rows, :], wd_v.at[rows, :], wd_s.at[n])

    def wgu_load(half, k):
        rows = pl.ds(pl.multiple_of(half * H, H), H)
        src = (wg, wu)[k]
        return pltpu.make_async_copy(src.at[rows, :], wgu_v.at[rows, pl.ds(k * F, F)], wgu_s.at[half, k])

    def to_partner(r):
        return pltpu.make_async_remote_copy(
            term_v.at[r], got_v.at[r], p1s.at[r], p1r.at[r], device_id={"tp": partner}, device_id_type=MESH)

    def to_across(r):
        return pltpu.make_async_remote_copy(
            sum_v.at[r], cross_v.at[r], xs.at[r], xr.at[r], device_id={"tp": across}, device_id_type=MESH)

    def dx_block(r):
        return dx_o.at[pl.ds(r * R, R), pl.ds(pl.multiple_of(core * H, H), H)]

    def share(r):
        return pltpu.make_async_remote_copy(
            sum_v.at[r], dx_block(r), p3s.at[r], p3r.at[r], device_id={"tp": partner}, device_id_type=MESH)

    def keep(r):
        return pltpu.make_async_copy(sum_v.at[r], dx_block(r), f_s.at[r])

    def put_late(r):
        rows = pl.ds(pl.multiple_of((r - NX) * R, R), R)
        return pltpu.make_async_copy(sum_v.at[r], late_o.at[rows, :], late_s.at[r])

    def epilogue(slot, out):
        for i in range(0, R, 16):
            for j in range(0, F, 512):
                at = (pl.ds(i, 16), pl.ds(j, 512))
                dh = acc[at]
                g = g_v[(slot, *at)].astype(jnp.float32)
                u = u_v[(slot, *at)].astype(jnp.float32)
                sig = 1.0 / (1.0 + jnp.exp(-g))
                silu = g * sig
                hid_v[(out, *at)] = (silu * u).astype(BF)
                dgu_v[(out, pl.ds(i, 16), pl.ds(j, 512))] = ((dh * u) * (sig * (1.0 + g * (1.0 - sig)))).astype(BF)
                dgu_v[(out, pl.ds(i, 16), pl.ds(F + j, 512))] = (dh * silu).astype(BF)

    def term(slot, half):
        rows = pl.ds(pl.multiple_of(half * H, H), H)
        return dot(dgu_v[slot], wgu_v[rows, :], NT)

    def finish(r):
        to_across(r).wait()
        sum_v[r] = (sum_v[r].astype(jnp.float32) + cross_v[r].astype(jnp.float32)).astype(BF)
        share(r).start()
        keep(r).start()

    for c in load(0, 0)[:1] + [wd_load(n) for n in range(4)] + load(0, 0)[1:]:
        c.start()
    barrier = pltpu.get_barrier_semaphore()
    for other in (partner, across):
        pl.semaphore_signal(barrier, inc=1, device_id={"tp": other}, device_id_type=MESH)
    pl.semaphore_wait(barrier, 2)

    load(0, 0)[0].wait()
    for n in range(4):
        wd_load(n).wait()
        if n == 2:
            for k in range(2):
                wgu_load(1 - core, k).start()
        if n == 3:
            for c in load(1, 1):
                c.start()
            for k in range(2):
                wgu_load(core, k).start()
        acc[:, pl.ds(n * 512, 512)] = dot(dy_v[0], wd_v[pl.ds(n * 512, 512), :], NT)
    for c in load(0, 0)[1:]:
        c.wait()
    epilogue(0, 0)
    for c in store(0, 0) + load(2, 0):
        c.start()
    for c in load(1, 1):
        c.wait()
    acc[...] = dot(dy_v[1], wd_v[...], NT)
    epilogue(1, 1)
    for c in store(1, 1) + load(3, 1):
        c.start()
    for k in range(2):
        wgu_load(1 - core, k).wait()
    term_v[0] = term(0, 1 - core).astype(BF)
    to_partner(0).start()
    for k in range(2):
        wgu_load(core, k).wait()

    def step(r, _):
        new, slot = lax.rem(r + 2, 3), lax.rem(r, 2)
        for c in load(r + 2, slot):
            c.wait()

        @pl.when(r >= 1)
        def _():
            for c in store(r - 1, new):
                c.wait()

        acc[...] = dot(dy_v[slot], wd_v[...], NT)
        to_partner(r).wait_recv()
        sum_v[r] = (term(lax.rem(r, 3), core) + got_v[r].astype(jnp.float32)).astype(BF)
        epilogue(slot, new)
        term_v[r + 1] = term(lax.rem(r + 1, 3), 1 - core).astype(BF)
        to_partner(r + 1).start()

        @pl.when(r < NX)
        def _():
            to_across(r).start()

        @pl.when(r >= NX)
        def _():
            put_late(r).start()

        for c in store(r + 2, new):
            c.start()

        @pl.when(r + 4 < C)
        def _():
            for c in load(r + 4, slot):
                c.start()

        for at, q in DONE_AT.items():
            @pl.when(r == at)
            def _():
                finish(q)
        return 0

    lax.fori_loop(0, C - 2, step, 0)

    r = C - 2
    to_partner(r).wait_recv()
    sum_v[r] = (term(r % 3, core) + got_v[r].astype(jnp.float32)).astype(BF)
    term_v[r + 1] = term((r + 1) % 3, 1 - core).astype(BF)
    to_partner(r + 1).start()
    put_late(r).start()
    for q in range(NX):
        if q not in DONE_AT.values():
            finish(q)
    r = C - 1
    to_partner(r).wait_recv()
    sum_v[r] = (term(r % 3, core) + got_v[r].astype(jnp.float32)).astype(BF)
    put_late(r).start()

    for q in range(NX):
        share(q).wait()
        keep(q).wait()
    for q in range(NX, C):
        put_late(q).wait()
    for q in range(C):
        to_partner(q).wait_send()
    for q in range(C - 3, C):
        for c in store(q, q % 3):
            c.wait()


def back(dy, gate, up, wd, wg, wu):
    hbm = pl.BlockSpec(memory_space=pl.ANY)
    full = jax.ShapeDtypeStruct((ROWS, F), BF)
    dma = pltpu.SemaphoreType.DMA
    return pl.pallas_call(
        back_kernel,
        in_specs=[hbm] * 6,
        out_specs=[hbm] * 5,
        out_shape=[full, full, full, jax.ShapeDtypeStruct((NX * R, D), BF), jax.ShapeDtypeStruct((LATE, H), BF)],
        scratch_shapes=[
            pltpu.VMEM((F, D), BF),
            pltpu.VMEM((D, 2 * F), BF),
            pltpu.VMEM((2, R, D), BF),
            pltpu.VMEM((2, R, F), BF),
            pltpu.VMEM((2, R, F), BF),
            pltpu.VMEM((R, F), jnp.float32),
            pltpu.VMEM((3, R, 2 * F), BF),
            pltpu.VMEM((3, R, F), BF),
            pltpu.VMEM((C, R, H), BF),
            pltpu.VMEM((C, R, H), BF),
            pltpu.VMEM((C, R, H), BF),
            pltpu.VMEM((NX, R, H), BF),
            dma((4,)), dma((2, 2)), dma((2, 3)), dma((3, 3)), dma((C,)), dma((C,)), dma((NX,)), dma((NX,)),
            dma((NX,)), dma((NX,)), dma((NX,)), dma((C,)),
        ],
        compiler_params=pltpu.CompilerParams(collective_id=0, has_side_effects=True, vmem_limit_bytes=66_900_000),
        cost_estimate=pl.CostEstimate(flops=6 * ROWS * D * F, bytes_accessed=90_000_000, transcendentals=ROWS * F),
        name="back",
    )(dy, gate, up, wd, wg, wu)


B = 1024
FIRST = {0: (0, 2), 1: (3,), 2: (1,), 4: (4,), 5: (5,), 8: (6, 8), 9: (9,), 10: (7,)}


def weights_kernel(x, dg, du, hid, dy, dx_e, dwg, dwu, dwd, dx_o, panel, out, early, panel_s, out_s, early_s):
    arrays = (x, dg, du, hid, dy)

    def panel_load(p):
        return pltpu.make_async_copy(arrays[p // 2].at[:, pl.ds((p % 2) * B, B)], panel.at[p], panel_s.at[p])

    def put(t, slot, ref):
        i, j = lax.rem(t, 4) // 2, lax.rem(t, 2)
        at = ref.at[pl.ds(pl.multiple_of(i * B, B), B), pl.ds(pl.multiple_of(j * B, B), B)]
        return pltpu.make_async_copy(out.at[slot], at, out_s.at[slot])

    def take():
        return pltpu.make_async_copy(dx_e, early, early_s.at[0])

    def give():
        return pltpu.make_async_copy(early, dx_o.at[pl.ds(0, NX * R), :], early_s.at[1])

    for p in FIRST[0]:
        panel_load(p).start()

    def step(t, _):
        for at, ps in FIRST.items():
            @pl.when(t == at)
            def _():
                for p in ps:
                    panel_load(p).wait()

            if at:
                @pl.when(t == max(at - 2, 0))
                def _():
                    for p in ps:
                        panel_load(p).start()

        @pl.when(t == 4)
        def _():
            take().start()

        @pl.when(t == 6)
        def _():
            take().wait()
            give().start()

        slot = lax.rem(t, 2)

        @pl.when(t >= 2)
        def _():
            put(t, slot, dwg).wait()

        left = t // 8 * 6 + lax.rem(t, 4) // 2
        right = 2 + t // 4 * 2 + t // 8 * 2 + lax.rem(t, 2)
        out[slot] = dot(panel[left], panel[right], TN).astype(BF)
        for k, ref in enumerate((dwg, dwu, dwd)):
            @pl.when(t // 4 == k)
            def _():
                put(t, slot, ref).start()
        return 0

    lax.fori_loop(0, 12, step, 0)
    put(10, 0, dwd).wait()
    put(11, 1, dwd).wait()
    give().wait()


def weights(x, dg, du, hid, dy, dx_e):
    hbm = pl.BlockSpec(memory_space=pl.ANY)
    full = jax.ShapeDtypeStruct((ROWS, F), BF)
    dma = pltpu.SemaphoreType.DMA
    return pl.pallas_call(
        weights_kernel,
        in_specs=[hbm] * 6,
        out_specs=[hbm] * 4,
        out_shape=[full] * 4,
        scratch_shapes=[
            pltpu.VMEM((10, ROWS, B), BF),
            pltpu.VMEM((2, B, B), BF),
            pltpu.VMEM((NX * R, D), BF),
            dma((10,)), dma((2,)), dma((2,)),
        ],
        compiler_params=pltpu.CompilerParams(vmem_limit_bytes=66_900_000),
        cost_estimate=pl.CostEstimate(flops=6 * ROWS * D * F, bytes_accessed=70_000_000, transcendentals=0),
        name="weights",
    )(x, dg, du, hid, dy, dx_e)


def join_kernel(mine, theirs, dx_in, dx_o):
    core = lax.rem(lax.axis_index("tp"), 2)
    a, b = mine[...], theirs[...]
    dx_o[:, pl.ds(0, H)] = jnp.where(core == 0, a, b)
    dx_o[:, pl.ds(H, H)] = jnp.where(core == 0, b, a)


def join(mine, theirs, dx):
    half = pl.BlockSpec((R, H), lambda i: (i, 0))
    return pl.pallas_call(
        join_kernel,
        grid=(C - NX,),
        in_specs=[half, half, pl.BlockSpec(memory_space=pl.ANY)],
        out_specs=pl.BlockSpec((R, D), lambda i: (i + NX, 0)),
        out_shape=jax.ShapeDtypeStruct((ROWS, D), BF),
        input_output_aliases={2: 0},
        name="join",
    )(mine, theirs, dx)


def solution(mesh):
    def step(x, dy, gate, up, w_gate, w_up, w_down):
        dg, du, hid, dx_e, late = back(dy, gate, up, w_down, w_gate, w_up)
        crossed = lax.ppermute(late, "tp", [(i, i ^ 2) for i in range(4)])
        dwg, dwu, dwd, dx = weights(x, dg, du, hid, dy, dx_e)
        crossed, dx = lax.optimization_barrier((crossed, dx))
        mine = (late.astype(jnp.float32) + crossed.astype(jnp.float32)).astype(BF)
        theirs = lax.ppermute(mine, "tp", [(i, i ^ 1) for i in range(4)])
        return join(mine, theirs, dx), dwg, dwu, dwd

    tokens, columns, rows = P("dp", None), P(None, "tp"), P("tp", None)
    return jax.shard_map(
        step,
        mesh=mesh,
        in_specs=(tokens, tokens, P("dp", "tp"), P("dp", "tp"), columns, columns, rows),
        out_specs=(tokens, P("dp", "tp"), P("dp", "tp"), P(("dp", "tp"), None)),
        check_vma=False,
    )
```

time: 256 us -> 155 us (0.61)
  matrix products: 156 us -> 0 us
  Pallas kernels: 0 us -> 144 us
  waiting for transfers between devices: 51.6 us -> 4.85 us
  local copies, waits for them, and re-layouts: 32.9 us -> 0.01 us
  between operations: 14 us -> 0.68 us
  other arithmetic: 0 us -> 3.78 us
    dot_general x6 -> x0, matrix products: 156 us -> none  [the longest x1 32.5 us: step(): d_hidden = jnp.dot(dy, w_down.T, preferred_element_type=jnp.float32)]
    pallas_call x0 -> x3, Pallas kernels: none -> 144 us  [the longest x1 77.5 us: back(): pl.pallas_call(back_kernel, in_specs=[hbm] * 6, out_specs=[hbm] * 5, out_...]
    psum x1 -> x0, waiting for transfers between devices: 51.6 us -> none  [step(): dx = lax.psum(term.astype(jnp.bfloat16), 'tp')]
    unnamed x3 -> x2, local copies, waits for them, and re-layouts: 32.9 us -> 0.01 us
    ppermute x0 -> x2, waiting for transfers between devices: none -> 4.85 us  [the longest x1 4.84 us: step(): theirs = lax.ppermute(mine, 'tp', [(i, i ^ 1) for i in range(4)])]
    convert_element_type x0 -> x1, other arithmetic: none -> 3.78 us  [step(): mine = (late.astype(jnp.float32) + crossed.astype(jnp.float32)).astype(BF)]
  transfers between devices with their start and end apart: 1 -> 2, of which waited for: 1 -> 1; matrix products, arithmetic and copies ran while one was open for 39% -> 0% of each run, Pallas kernels for 0% -> 39%
where the time goes in v1:
time: 155 us
  Pallas kernels  144 us (93%)
  waiting for transfers between devices  4.85 us (3%)
  other arithmetic  3.78 us (2%)
  starting transfers between devices  1.79 us (1%)
    pallas_call x1, Pallas kernels, back(): pl.pallas_call(back_kernel, in_specs=[hbm] * 6, out_specs=[hbm] * 5, out_...  77.5 us
    pallas_call x1, Pallas kernels, weights(): pl.pallas_call(weights_kernel, in_specs=[hbm] * 6, out_specs=[hbm] * 4, o...  59.6 us
    pallas_call x1, Pallas kernels, join(): pl.pallas_call(join_kernel, grid=(C - NX,), in_specs=[half, half, pl.Bloc...  6.48 us
    ppermute x1, waiting for transfers between devices, step(): theirs = lax.ppermute(mine, 'tp', [(i, i ^ 1) for i in range(4)])  4.84 us
    convert_element_type x1, other arithmetic, step(): mine = (late.astype(jnp.float32) + crossed.astype(jnp.float32)).astype(BF)  3.78 us
  transfers between devices with their start and end apart: 2, of which 1 were waited for; matrix products, arithmetic and copies ran while one was open for 0% of the time, Pallas kernels for 39%

profile of v1, /device:TPU:0, one launch (start us, length us, event | category | flops | bytes accessed | tf_op | source)
XLA Modules:
  0.0 154.7 jit_solution(18180190748494009774)
XLA Ops:
  0.6 77.5 %back.1 = (bf16[2048,2048]{1,0:T(8,128)(2,1)}, bf16[2048,2048]{1,0:T(8,128)(2,1)}, bf16[2048,2048]{1,0:T(8,128)(2,1)}, bf16[768,2048]{1,0:T(8,128)(2,1)}, bf16[1280,1024]{1,0:T(8,128)(2,1)}) custom-call(bf16[2048,2048]{1,0:T(8,128)(2,1)} %dy.3, bf16[2048,2048]{1,0:T(8,128)(2,1)} %gate.1, bf16[2048,2048]{1,0:T(8,128)(2,1)} %up.1, bf16[2048,2048]{1,0:T(8,128)(2,1)} %wd.1, ...), custom_call_target="tpu_custom_call" | custom-call | flops 51539607552 | bytes 90000000 | tf_op jit(solution)/shard_map/back/pallas_call | solution.py:215
  78.2 1.8 %collective-permute-start = (bf16[1280,1024]{1,0:T(8,128)(2,1)}, bf16[1280,1024]{1,0:T(8,128)(2,1)}, u32[]{:S(2)}, u32[]{:S(2)}) collective-permute-start(bf16[1280,1024]{1,0:T(8,128)(2,1)} %get-tuple-element.15), channel_id=1, source_target_pairs={{0,2},{1,3},{2,0},{3,1},{4,6},{5,7},{6,4},{7,5}} | collective-permute-start | bytes 7864328 | tf_op jit(solution)/shard_map/ppermute | solution.py:353
  79.9 59.6 %weights.1 = (bf16[2048,2048]{1,0:T(8,128)(2,1)}, bf16[2048,2048]{1,0:T(8,128)(2,1)}, bf16[2048,2048]{1,0:T(8,128)(2,1)}, bf16[2048,2048]{1,0:T(8,128)(2,1)}) custom-call(bf16[2048,2048]{1,0:T(8,128)(2,1)} %x.1, bf16[2048,2048]{1,0:T(8,128)(2,1)} %get-tuple-element.16.dg, bf16[2048,2048]{1,0:T(8,128)(2,1)} %get-tuple-element.17.du, ...), custom_call_target="tpu_custom_call" | custom-call | flops 51539607552 | bytes 70000000 | tf_op jit(solution)/shard_map/weights/pallas_call | solution.py:313
  139.5 0.0 collective-permute-done
  139.5 3.8 %add_convert_fusion.mine = bf16[1280,1024]{1,0:T(8,128)(2,1)S(1)} fusion(bf16[1280,1024]{1,0:T(8,128)(2,1)} %collective-permute-done, bf16[1280,1024]{1,0:T(8,128)(2,1)} %get-tuple-element.15), kind=kLoop, calls=%fused_computation | loop fusion | flops 5242880 | bytes 7864320 | tf_op jit(solution)/shard_map/convert_element_type | solution.py:356
  143.3 0.0 copy-start
  143.3 0.0 collective-permute-start.1
  143.3 4.8 %collective-permute-done.1.theirs = bf16[1280,1024]{1,0:T(8,128)(2,1)} collective-permute-done((bf16[1280,1024]{1,0:T(8,128)(2,1)S(1)}, bf16[1280,1024]{1,0:T(8,128)(2,1)}, u32[]{:S(2)}, u32[]{:S(2)}) %collective-permute-start.1) | collective-permute-done | bytes 2621472 | tf_op jit(solution)/shard_map/ppermute | solution.py:357
  148.2 0.0 copy-done
  148.2 6.5 %join.1 = bf16[2048,2048]{1,0:T(8,128)(2,1)} custom-call(bf16[1280,1024]{1,0:T(8,128)(2,1)} %copy-done, bf16[1280,1024]{1,0:T(8,128)(2,1)} %collective-permute-done.1.theirs, bf16[2048,2048]{1,0:T(8,128)(2,1)} %get-tuple-element.22.dx_in), custom_call_target="tpu_custom_call", output_to_operand_aliasing={{}: (2, {})} | custom-call | tf_op jit(solution)/shard_map/join/pallas_call | solution.py:339
Async XLA Ops:
  78.2 61.3 %collective-permute-start = (bf16[1280,1024]{1,0:T(8,128)(2,1)}, bf16[1280,1024]{1,0:T(8,128)(2,1)}, u32[]{:S(2)}, u32[]{:S(2)}) collective-permute-start(bf16[1280,1024]{1,0:T(8,128)(2,1)} %get-tuple-element.15), channel_id=1, source_target_pairs={{0,2},{1,3},{2,0},{3,1},{4,6},{5,7},{6,4},{7,5}} | collective-permute-start | bytes 7864328 | tf_op jit(solution)/shard_map/ppermute | solution.py:353
  143.3 4.9 %copy-start = (bf16[1280,1024]{1,0:T(8,128)(2,1)}, bf16[1280,1024]{1,0:T(8,128)(2,1)S(1)}, u32[]{:S(2)}) copy-start(bf16[1280,1024]{1,0:T(8,128)(2,1)S(1)} %add_convert_fusion.mine) | copy-start | bytes 7864324
  143.3 4.9 %collective-permute-start.1 = (bf16[1280,1024]{1,0:T(8,128)(2,1)S(1)}, bf16[1280,1024]{1,0:T(8,128)(2,1)}, u32[]{:S(2)}, u32[]{:S(2)}) collective-permute-start(bf16[1280,1024]{1,0:T(8,128)(2,1)S(1)} %add_convert_fusion.mine), channel_id=1, source_target_pairs={{0,1},{1,0},{2,3},{3,2},{4,5},{5,4},{6,7},{7,6}} | collective-permute-start | bytes 7864328 | tf_op jit(solution)/shard_map/ppermute | solution.py:357
